TPU v7x, 128 devices: a whole 4x4x4 slice. The times are simulated.
128 devices in a mesh: branch: 4 (over z_lo, core), shard: 32 (over y, x, z_hi).
Axes of the slice: x: 4, y: 4, z: 4 (z_hi: 2, z_lo: 2; z = z_hi * 2 + z_lo), core: 2. Of those that a mesh axis runs over, the one named last changes fastest.
Arguments:
- attention_weights: bfloat16 [4, 2, 4096, 4096], P('branch', None, None, 'shard'), may hold values from -1.25 to 1.25
- ffn_weights: bfloat16 [4, 3, 4096, 11008], P('branch', None, 'shard'), may hold values from -0.3125 to 0.3125
- tokens: bfloat16 [2048, 4096], P(('branch', 'shard')), may hold values from -6 to 6
- routes: int32 [2048, 2], P(('branch', 'shard')), may hold values from 0 to 3, all different within a row; in each aligned block of 16 rows (0 to 15, 16 to 31, ...) at most 12 rows name the same one
- router: bfloat16 [4096, 4], replicated, may hold values from -0.09375 to 0.09375
Outputs:
- merged_attention: bfloat16 [2, 4096, 4096], P(None, 'branch', 'shard')
- expert_weights: bfloat16 [4, 3, 4096, 11008], P('branch', None, None, 'shard')
- mixed_output: bfloat16 [2048, 4096], P(('branch', 'shard'))
Inputs may be any that keep to these rules, and one draw needn't show every extreme that they name: `routes`: the 2 experts of a row differ. In each aligned block of 16 rows (the rows of one device) no expert is named by more than 12 rows, and in some blocks one expert is named by exactly 12 rows.
All inputs are finite; a program needn't handle non-finite values.
Results may differ from a plain program's by a relative error of at most 0.018.
Values may be sent and summed in bfloat16 or wider, within the bound.
A program may use at most 192 MiB of HBM per device.

v0:
```python
import jax
import jax.numpy as jnp
from jax import lax
from jax.sharding import Mesh
from jax.sharding import PartitionSpec as P

SHARD = ("shard_0", "shard_1", "shard_2")
BRANCH_SHARD = ("branch", "shard_0", "shard_1", "shard_2")


def own_rows(terms, axes):
    running = terms.astype(jnp.bfloat16)
    for axis in axes:
        running = lax.psum_scatter(running, axis, scatter_dimension=0, tiled=True)
    return running.astype(jnp.float32)


def slot_table(route_rows, experts_count, capacity):
    chosen = (route_rows[:, :, None] == jnp.arange(experts_count, dtype=jnp.int32)).astype(
        jnp.int32
    )
    flat_picks = chosen.reshape(-1, experts_count)
    before = jnp.cumsum(flat_picks, axis=0) - flat_picks
    position = jnp.sum(before * flat_picks, axis=1)
    slot_id = route_rows.reshape(-1) * capacity + position
    one_hot = (slot_id[:, None] == jnp.arange(experts_count * capacity, dtype=jnp.int32)).astype(
        jnp.float32
    )
    return jnp.sum(one_hot.reshape(route_rows.shape[0], route_rows.shape[1], -1), axis=1)


def local(attention_weights, ffn_weights, tokens, routes, router):
    branches = lax.axis_size("branch")
    expert_weights = lax.all_to_all(ffn_weights, SHARD, split_axis=3, concat_axis=2, tiled=True)
    gate_weight = expert_weights[0, 0]
    up_weight = expert_weights[0, 1]
    down_weight = expert_weights[0, 2]
    tok_count = tokens.shape[0]
    model_width = tokens.shape[1]
    capacity = 3 * tok_count // 4
    slot_map = slot_table(routes, branches, capacity)
    buffers = lax.dot_general(
        slot_map.astype(jnp.bfloat16),
        tokens,
        (((0,), (0,)), ((), ())),
        preferred_element_type=jnp.float32,
    )
    buffers = buffers.astype(jnp.bfloat16).reshape(branches, capacity, model_width)
    arrived = lax.all_to_all(buffers, "branch", split_axis=0, concat_axis=0, tiled=True)
    slot_rows = lax.all_gather(
        arrived.reshape(branches * capacity, model_width), SHARD, axis=0, tiled=True
    )
    gate_proj = jnp.dot(slot_rows, gate_weight, preferred_element_type=jnp.float32)
    up_proj = jnp.dot(slot_rows, up_weight, preferred_element_type=jnp.float32)
    hidden = (jax.nn.silu(gate_proj) * up_proj).astype(jnp.bfloat16)
    summed = own_rows(
        lax.dot_general(
            hidden, down_weight, (((1,), (1,)), ((), ())), preferred_element_type=jnp.float32
        ),
        SHARD,
    )
    outputs = summed.astype(jnp.bfloat16).reshape(branches, capacity, model_width)
    returned = lax.all_to_all(outputs, "branch", split_axis=0, concat_axis=0, tiled=True)
    gates_all = jax.nn.sigmoid(jnp.dot(tokens, router, preferred_element_type=jnp.float32))
    weighting = slot_map * jnp.repeat(gates_all, capacity, axis=1)
    mixed_output = jnp.dot(
        weighting, returned.reshape(branches * capacity, model_width).astype(jnp.float32)
    )
    mixed_output = mixed_output.astype(jnp.bfloat16)
    traded = lax.all_to_all(attention_weights, "branch", split_axis=2, concat_axis=0, tiled=True)
    summed_attention = jnp.sum(traded.astype(jnp.float32), axis=0)
    merged_attention = (summed_attention * (1.0 / branches)).astype(jnp.bfloat16)
    return (merged_attention, expert_weights, mixed_output)


def solution(mesh):
    torus = Mesh(
        mesh.devices.reshape(mesh.shape["branch"], 4, 4, 2),
        ("branch", "shard_0", "shard_1", "shard_2"),
    )
    in_specs = (
        P("branch", None, None, SHARD),
        P("branch", None, SHARD, None),
        P(BRANCH_SHARD, None),
        P(BRANCH_SHARD, None),
        P(),
    )
    out_specs = (P(None, "branch", SHARD), P("branch", None, None, SHARD), P(BRANCH_SHARD, None))
    return jax.shard_map(local, mesh=torus, in_specs=in_specs, out_specs=out_specs, check_vma=False)
```

profile of v0, /device:TPU:1, one launch (start us, length us, event | category | flops | bytes accessed | tf_op | source)
XLA Modules:
  0.0 518.2 jit_solution(2717877055317344785)
XLA Ops:
  7.2 0.0 copy-start
  7.2 0.0 all-gather.2.cloned.1.call-start
  7.2 0.8 copy.58
  8.0 0.1 eq.30
  8.1 0.1 fusion.13
  8.2 0.1 reduce_window_sum.11
  8.2 0.2 select_reduce_fusion
  8.4 0.1 reduce_sum.33
  8.5 0.1 copy.59
  8.6 0.7 multiply_add_fusion
  9.3 0.1 convert_reduce_fusion.1
  9.4 0.0 copy-done
  9.4 0.3 convolution_convert_fusion.1
  9.7 0.1 reshape.45
  9.8 12.2 %all_to_all.37 = bf16[4,12,4096]{2,1,0:T(8,128)(2,1)S(1)} all-to-all(bf16[4,12,4096]{2,1,0:T(8,128)(2,1)S(1)} %reshape.45), channel_id=1, replica_groups=mesh['branch'=4,'shard_0'=4,'shard_1'=4,'shard_2'=2] {'branch'}, dimensions={0} | all-to-all | bytes 786432 | tf_op jit(solution)/shard_map/all_to_all | solution.py:49
  22.0 0.8 reshape.46
  22.8 0.0 all-gather.2.cloned.1.call-update
  22.9 0.0 reduce-scatter.4.cloned.1.call-start
  22.9 17.6 %copy.55 = bf16[1,3,128,11008]{2,1,0,3:T(4,128)(2,1)} copy(bf16[1,3,128,11008]{3,2,1,0:T(8,128)(2,1)} %param.6) | data formatting | bytes 16908288 | tf_op args[1]
  40.5 145.7 %all_to_all.38 = bf16[1,3,128,11008]{2,1,0,3:T(4,128)(2,1)S(1)} all-to-all(bf16[1,3,128,11008]{2,1,0,3:T(4,128)(2,1)} %copy.55), channel_id=1, replica_groups=mesh['branch'=4,'shard_0'=4,'shard_1'=4,'shard_2'=2] {'shard_0','shard_1..., dimensions={3} | all-to-all | bytes 16908288 | tf_op jit(solution)/shard_map/all_to_all | solution.py:34
  186.2 5.0 copy.56
  191.3 9.2 %copy.67 = bf16[1,3,32,43,8,128]{5,4,2,3,1,0:T(8,128)(2,1)} copy(bf16[1,3,32,43,8,128]{5,4,3,2,1,0:T(8,128)(2,1)} %bitcast.32) | data formatting | bytes 16908288 | tf_op jit(solution)/shard_map/all_to_all | solution.py:34
  200.4 67.3 %all-gather.2.cloned.1.call-done = bf16[1536,4096]{1,0:T(8,128)(2,1)} async-done(((bf16[48,4096]{1,0:T(8,128)(2,1)}), bf16[1536,4096]{1,0:T(8,128)(2,1)}) %all-gather.2.cloned.1.call-update) | async-done | bytes 12582928 | tf_op jit(solution)/shard_map/all_gather | solution.py:50
  267.7 8.5 %fusion.1 = f32[1536,344]{0,1:T(8,128)S(1)} fusion(bf16[1536,4096]{1,0:T(8,128)(2,1)} %all-gather.2.cloned.1.call-done, bf16[1,3,4096,344]{2,3,1,0:T(8,128)(2,1)} %bitcast.33), kind=kOutput, calls=%fused_computation.10 | convolution fusion | flops 4328521728 | bytes 17514496 | tf_op jit(solution)/shard_map/dot_general | solution.py:53
  276.2 21.6 %convolution_convert_fusion = bf16[1536,4096]{1,0:T(8,128)(2,1)} fusion(bf16[1,3,4096,344]{2,3,1,0:T(8,128)(2,1)} %bitcast.34, bf16[1536,4096]{1,0:T(8,128)(2,1)} %all-gather.2.cloned.1.call-done, f32[1536,344]{0,1:T(8,128)S(1)} %fusion.1), kind=kOutput, calls=%fused_computation | convolution fusion | flops 8666505216 | bytes 32915456 | tf_op jit(solution)/shard_map/dot_general | solution.py:57
  297.7 0.0 reduce-scatter.4.cloned.1.call-update
  297.7 0.0 copy-start.1
  297.8 0.0 reduce-scatter.6.cloned.1.call-start
  297.8 113.0 %reduce-scatter.4.cloned.1.call-done = bf16[384,4096]{1,0:T(8,128)(2,1)} async-done(((bf16[1536,4096]{1,0:T(8,128)(2,1)}), bf16[384,4096]{1,0:T(8,128)(2,1)}) %reduce-scatter.4.cloned.1.call-update) | async-done | bytes 3145744 | tf_op jit(solution)/shard_map/reduce_scatter | solution.py:14
  410.8 0.0 reduce-scatter.6.cloned.1.call-update
  410.8 0.2 reduce-scatter.8.cloned.1.call-start
  411.0 40.1 %reduce-scatter.6.cloned.1.call-done = bf16[96,4096]{1,0:T(8,128)(2,1)} async-done(((bf16[384,4096]{1,0:T(8,128)(2,1)}), bf16[96,4096]{1,0:T(8,128)(2,1)}) %reduce-scatter.6.cloned.1.call-update) | async-done | bytes 786448 | tf_op jit(solution)/shard_map/reduce_scatter | solution.py:14
  451.2 0.0 reduce-scatter.8.cloned.1.call-update
  451.2 0.0 copy-done.1
  451.2 18.1 %copy.54 = bf16[1,2,4096,128]{3,1,0,2:T(2,128)(2,1)} copy(bf16[1,2,4096,128]{3,2,1,0:T(8,128)(2,1)S(1)} %copy-done.1) | data formatting | bytes 4194304 | tf_op args[0]
  469.3 0.0 copy-start.2
  469.3 4.4 all-to-all-start
  473.8 0.1 reduce_sum.35
  473.8 0.0 copy-done.2
  473.9 0.2 fusion.10
  474.0 0.1 copy.60
  474.1 0.1 broadcast_multiply_fusion
  474.2 0.5 reduce-scatter.8.cloned.1.call-done
  474.8 1.9 reshape.47
  476.6 21.8 %all-to-all-done = bf16[1,2,4096,128]{3,1,0,2:T(2,128)(2,1)S(1)} async-done(((bf16[1,2,4096,128]{3,1,0,2:T(2,128)(2,1)}), bf16[1,2,4096,128]{3,1,0,2:T(2,128)(2,1)S(1)}, u32[]{:S(2)}, u32[]{:S(2)}) %all-to-all-start) | async-done | bytes 2097184 | tf_op jit(solution)/shard_map/all_to_all | solution.py:70
  498.5 4.4 all-to-all-start.3
  502.9 2.1 convert_reduce_fusion
  505.0 0.5 multiply_convert_fusion
  505.5 0.9 copy.62
  506.3 4.4 all-to-all-done.3
  510.7 1.0 fusion
Async XLA Ops:
  7.2 2.2 copy-start
  7.2 260.5 %all-gather.2.cloned.1.call-start = ((), (), s32[]{:S(2)}) async-start(), calls=%async_computation.7 | async-start | bytes 12976128 | tf_op jit(solution)/shard_map/all_gather | solution.py:50
  22.9 387.9 %reduce-scatter.4.cloned.1.call-start = ((), (), s32[]{:S(2)}) async-start(), calls=%async_computation.8 | async-start | bytes 15728640 | tf_op jit(solution)/shard_map/reduce_scatter | solution.py:14
  297.7 153.4 %copy-start.1 = (bf16[1,2,4096,128]{3,2,1,0:T(8,128)(2,1)S(1)}, bf16[1,2,4096,128]{3,2,1,0:T(8,128)(2,1)}, u32[]{:S(2)}) copy-start(bf16[1,2,4096,128]{3,2,1,0:T(8,128)(2,1)} %param.5) | copy-start | bytes 6291460
  297.8 153.4 %reduce-scatter.6.cloned.1.call-start = ((), (), s32[]{:S(2)}) async-start(), calls=%async_computation.9 | async-start | bytes 3932160 | tf_op jit(solution)/shard_map/reduce_scatter | solution.py:14
  410.8 64.0 %reduce-scatter.8.cloned.1.call-start = ((), (), s32[]{:S(2)}) async-start(), calls=%async_computation.10 | async-start | bytes 1179648 | tf_op jit(solution)/shard_map/reduce_scatter | solution.py:14
  469.3 4.5 copy-start.2
  469.3 29.1 %all-to-all-start = ((bf16[1,2,4096,128]{3,1,0,2:T(2,128)(2,1)}), bf16[1,2,4096,128]{3,1,0,2:T(2,128)(2,1)S(1)}, u32[]{:S(2)}, u32[]{:S(2)}) async-start(bf16[1,2,4096,128]{3,1,0,2:T(2,128)(2,1)} %copy.54), calls=%async_computation | async-start | bytes 4194304 | tf_op jit(solution)/shard_map/all_to_all | solution.py:70
  498.5 12.3 %all-to-all-start.3 = ((bf16[4,12,4096]{2,1,0:T(8,128)(2,1)}), bf16[4,12,4096]{2,1,0:T(8,128)(2,1)S(1)}, u32[]{:S(2)}, u32[]{:S(2)}) async-start(bf16[4,12,4096]{2,1,0:T(8,128)(2,1)} %reshape.47), calls=%async_computation.6 | async-start | bytes 1048576 | tf_op jit(solution)/shard_map/all_to_all | solution.py:63
Sparse Core Ops, SparseCore 0:
  23.0 244.6 all-gather.1
  297.9 112.8 reduce-scatter.3
  413.2 37.9 reduce-scatter.5
  453.4 21.3 reduce-scatter.7
where the time goes:
time: 519 us; the launch traced here: 518 us
  waiting for transfers between devices  247 us (48%)
  blocking collectives  158 us (30%)
  local copies, waits for them, and re-layouts  54.8 us (11%)
  matrix products  31.4 us (6%)
  between operations  13.9 us (3%)
  starting transfers between devices  9.18 us (2%)
    reduce_scatter x3, waiting for transfers between devices, own_rows(): running = lax.psum_scatter(running, axis, scatter_dimension=0, tiled=True)  154 us
    all_to_all x1, blocking collectives, local(): lax.all_to_all(ffn_weights, SHARD, split_axis=3, concat_axis=2, tiled=True)  146 us
    all_gather x1, waiting for transfers between devices, local(): lax.all_gather(arrived.reshape(branches * capacity, model_width), SHARD,...  67.3 us
    unnamed x10, local copies, waits for them, and re-layouts  37.4 us
    all_to_all x1, waiting for transfers between devices, local(): lax.all_to_all(attention_weights, 'branch', split_axis=2, concat_axis=0,...  21.8 us
    dot_general x1, matrix products, local(): lax.dot_general(hidden, down_weight, (((1,), (1,)), ((), ())), preferred_...  21.6 us
    all_to_all x2, local copies, waits for them, and re-layouts, local(): lax.all_to_all(ffn_weights, SHARD, split_axis=3, concat_axis=2, tiled=True)  14.2 us
    all_to_all x1, blocking collectives, local(): lax.all_to_all(buffers, 'branch', split_axis=0, concat_axis=0, tiled=True)  12.2 us
  transfers between devices with their start and end apart: 6, of which 6 were waited for; matrix products, arithmetic and copies ran while one was open for 11% of the time, Pallas kernels for 0%

commit v1 on v0

--- a/solution.py
+++ b/solution.py
@@ -47,8 +47,14 @@
     )
     buffers = buffers.astype(jnp.bfloat16).reshape(branches, capacity, model_width)
     arrived = lax.all_to_all(buffers, "branch", split_axis=0, concat_axis=0, tiled=True)
-    slot_rows = lax.all_gather(
-        arrived.reshape(branches * capacity, model_width), SHARD, axis=0, tiled=True
+    slot_rows = jnp.concatenate(
+        lax.all_to_all(
+            jnp.stack([arrived.reshape(branches * capacity, model_width)] * lax.axis_size(SHARD)),
+            SHARD,
+            0,
+            0,
+        ),
+        axis=0,
     )
     gate_proj = jnp.dot(slot_rows, gate_weight, preferred_element_type=jnp.float32)
     up_proj = jnp.dot(slot_rows, up_weight, preferred_element_type=jnp.float32)

time: 519 us -> 728 us (1.40)
  waiting for transfers between devices: 247 us -> 556 us
  blocking collectives: 158 us -> 0 us
  starting transfers between devices: 9.18 us -> 57.3 us
  local copies, waits for them, and re-layouts: 54.8 us -> 64.6 us
    all_to_all x0 -> x3, waiting for transfers between devices: none -> 347 us  [the longest x1 175 us: local(): lax.all_to_all(ffn_weights, SHARD, split_axis=3, concat_axis=2, tiled=True)]
    all_to_all x2 -> x0, blocking collectives: 158 us -> none  [the longest x1 146 us: local(): lax.all_to_all(ffn_weights, SHARD, split_axis=3, concat_axis=2, tiled=True)]
    all_gather x1 -> x0, waiting for transfers between devices: 67.3 us -> none  [local(): lax.all_gather(arrived.reshape(branches * capacity, model_width), SHARD,...]
    all_to_all x0 -> x3, starting transfers between devices: none -> 47.9 us  [the longest x1 32.5 us: local(): lax.all_to_all(jnp.stack([arrived.reshape(branches * capacity, model_widt...]
    reduce_scatter x3, waiting for transfers between devices: 154 us -> 183 us  [own_rows(): running = lax.psum_scatter(running, axis, scatter_dimension=0, tiled=True)]
  transfers between devices with their start and end apart: 6 -> 8, of which waited for: 6 -> 7; matrix products, arithmetic and copies ran while one was open for 11% -> 8% of each run, Pallas kernels for 0% -> 0%
where the time goes in v1:
time: 728 us; the launch traced here: 727 us
  waiting for transfers between devices  556 us (76%)
  local copies, waits for them, and re-layouts  64.6 us (9%)
  starting transfers between devices  57.3 us (8%)
  matrix products  31.4 us (4%)
  between operations  13.9 us (2%)
    reduce_scatter x3, waiting for transfers between devices, own_rows(): running = lax.psum_scatter(running, axis, scatter_dimension=0, tiled=True)  183 us
    all_to_all x1, waiting for transfers between devices, local(): lax.all_to_all(ffn_weights, SHARD, split_axis=3, concat_axis=2, tiled=True)  175 us
    all_to_all x1, waiting for transfers between devices, local(): lax.all_to_all(jnp.stack([arrived.reshape(branches * capacity, model_widt...  172 us
    unnamed x10, local copies, waits for them, and re-layouts  37.3 us
    all_to_all x1, starting transfers between devices, local(): lax.all_to_all(jnp.stack([arrived.reshape(branches * capacity, model_widt...  32.5 us
    all_to_all x1, waiting for transfers between devices, local(): lax.all_to_all(attention_weights, 'branch', split_axis=2, concat_axis=0,...  21.7 us
    dot_general x1, matrix products, local(): lax.dot_general(hidden, down_weight, (((1,), (1,)), ((), ())), preferred_...  21.6 us
    all_to_all x2, local copies, waits for them, and re-layouts, local(): lax.all_to_all(ffn_weights, SHARD, split_axis=3, concat_axis=2, tiled=True)  17.9 us
  transfers between devices with their start and end apart: 8, of which 7 were waited for; matrix products, arithmetic and copies ran while one was open for 8% of the time, Pallas kernels for 0%

profile of v1, /device:TPU:1, one launch (start us, length us, event | category | flops | bytes accessed | tf_op | source)
XLA Modules:
  0.0 726.6 jit_solution(15192647803113631676)
XLA Ops:
  7.2 0.0 copy-start
  7.2 0.8 copy.58
  8.0 0.1 eq.30
  8.1 0.1 fusion.13
  8.1 0.1 reduce_window_sum.11
  8.2 0.2 select_reduce_fusion
  8.4 0.1 reduce_sum.33
  8.5 0.1 copy.59
  8.5 0.7 multiply_add_fusion
  9.2 0.1 convert_reduce_fusion.1
  9.3 0.0 copy-done
  9.3 0.3 convolution_convert_fusion.1
  9.6 0.9 reshape.47
  10.5 4.8 all-to-all-start.2
  15.3 17.5 %copy.55 = bf16[1,3,128,11008]{2,1,0,3:T(4,128)(2,1)} copy(bf16[1,3,128,11008]{3,2,1,0:T(8,128)(2,1)} %param.6) | data formatting | bytes 16908288 | tf_op args[1]
  32.9 0.0 all-to-all-done.2
  32.9 10.6 %all-to-all-start.1 = ((bf16[1,3,128,11008]{2,1,0,3:T(4,128)(2,1)}), bf16[1,3,128,11008]{2,1,0,3:T(4,128)(2,1)}, u32[]{:S(2)}, u32[]{:S(2)}) async-start(bf16[1,3,128,11008]{2,1,0,3:T(4,128)(2,1)} %copy.55), calls=%async_computation.1 | async-start | bytes 22544384 | tf_op jit(solution)/shard_map/all_to_all | solution.py:34
  43.4 0.1 stack_reshape.2
  43.5 175.2 %all-to-all-done.1 = bf16[1,3,128,11008]{2,1,0,3:T(4,128)(2,1)} async-done(((bf16[1,3,128,11008]{2,1,0,3:T(4,128)(2,1)}), bf16[1,3,128,11008]{2,1,0,3:T(4,128)(2,1)}, u32[]{:S(2)}, u32[]{:S(2)}) %all-to-all-start.1) | async-done | bytes 8454176 | tf_op jit(solution)/shard_map/all_to_all | solution.py:34
  218.7 6.0 stack.3
  224.7 32.5 %all-to-all-start.3 = ((bf16[32,48,4096]{2,1,0:T(8,128)(2,1)}), bf16[32,48,4096]{2,1,0:T(8,128)(2,1)}, u32[]{:S(2)}, u32[]{:S(2)}) async-start(bf16[32,48,4096]{2,1,0:T(8,128)(2,1)} %stack.3), calls=%async_computation.3 | async-start | bytes 25165824 | tf_op jit(solution)/shard_map/all_to_all | solution.py:51
  257.2 0.2 reduce-scatter.4.cloned.1.call-start
  257.5 8.8 %copy.56 = bf16[1,3,128,11008]{2,3,1,0:T(8,128)(2,1)} copy(bf16[1,3,128,11008]{2,1,0,3:T(4,128)(2,1)} %all-to-all-done.1) | data formatting | bytes 16908288 | tf_op jit(solution)/shard_map/all_to_all | solution.py:34
  266.2 9.2 %copy.67 = bf16[1,3,32,43,8,128]{5,4,2,3,1,0:T(8,128)(2,1)} copy(bf16[1,3,32,43,8,128]{5,4,3,2,1,0:T(8,128)(2,1)} %bitcast.33) | data formatting | bytes 16908288 | tf_op jit(solution)/shard_map/all_to_all | solution.py:34
  275.4 171.9 %all-to-all-done.3 = bf16[32,48,4096]{2,1,0:T(8,128)(2,1)} async-done(((bf16[32,48,4096]{2,1,0:T(8,128)(2,1)}), bf16[32,48,4096]{2,1,0:T(8,128)(2,1)}, u32[]{:S(2)}, u32[]{:S(2)}) %all-to-all-start.3) | async-done | bytes 12582944 | tf_op jit(solution)/shard_map/all_to_all | solution.py:51
  447.3 8.5 %fusion.1 = f32[1536,344]{0,1:T(8,128)S(1)} fusion(bf16[1536,4096]{1,0:T(8,128)(2,1)} %bitcast.3, bf16[1,3,4096,344]{2,3,1,0:T(8,128)(2,1)} %bitcast.34), kind=kOutput, calls=%fused_computation.10 | convolution fusion | flops 4328521728 | bytes 17514496 | tf_op jit(solution)/shard_map/dot_general | solution.py:59
  455.8 21.6 %convolution_convert_fusion = bf16[1536,4096]{1,0:T(8,128)(2,1)} fusion(bf16[1,3,4096,344]{2,3,1,0:T(8,128)(2,1)} %bitcast.35, bf16[1536,4096]{1,0:T(8,128)(2,1)} %bitcast.3, f32[1536,344]{0,1:T(8,128)S(1)} %fusion.1), kind=kOutput, calls=%fused_computation | convolution fusion | flops 8666505216 | bytes 32915456 | tf_op jit(solution)/shard_map/dot_general | solution.py:63
  477.4 0.0 reduce-scatter.4.cloned.1.call-update
  477.4 0.0 copy-start.1
  477.4 0.0 reduce-scatter.6.cloned.1.call-start
  477.5 141.7 %reduce-scatter.4.cloned.1.call-done = bf16[384,4096]{1,0:T(8,128)(2,1)} async-done(((bf16[1536,4096]{1,0:T(8,128)(2,1)}), bf16[384,4096]{1,0:T(8,128)(2,1)}) %reduce-scatter.4.cloned.1.call-update) | async-done | bytes 3145744 | tf_op jit(solution)/shard_map/reduce_scatter | solution.py:14
  619.2 0.0 reduce-scatter.6.cloned.1.call-update
  619.2 0.3 reduce-scatter.8.cloned.1.call-start
  619.5 40.1 %reduce-scatter.6.cloned.1.call-done = bf16[96,4096]{1,0:T(8,128)(2,1)} async-done(((bf16[384,4096]{1,0:T(8,128)(2,1)}), bf16[96,4096]{1,0:T(8,128)(2,1)}) %reduce-scatter.6.cloned.1.call-update) | async-done | bytes 786448 | tf_op jit(solution)/shard_map/reduce_scatter | solution.py:14
  659.6 0.0 reduce-scatter.8.cloned.1.call-update
  659.6 0.0 copy-done.1
  659.6 18.1 %copy.54 = bf16[1,2,4096,128]{3,1,0,2:T(2,128)(2,1)} copy(bf16[1,2,4096,128]{3,2,1,0:T(8,128)(2,1)S(1)} %copy-done.1) | data formatting | bytes 4194304 | tf_op args[0]
  677.7 0.0 copy-start.2
  677.7 4.4 all-to-all-start
  682.2 0.1 reduce_sum.35
  682.2 0.0 copy-done.2
  682.3 0.2 fusion.10
  682.4 0.1 copy.60
  682.5 0.1 broadcast_multiply_fusion
  682.6 0.7 reduce-scatter.8.cloned.1.call-done
  683.3 1.9 reshape.49
  685.2 21.7 %all-to-all-done = bf16[1,2,4096,128]{3,1,0,2:T(2,128)(2,1)S(1)} async-done(((bf16[1,2,4096,128]{3,1,0,2:T(2,128)(2,1)}), bf16[1,2,4096,128]{3,1,0,2:T(2,128)(2,1)S(1)}, u32[]{:S(2)}, u32[]{:S(2)}) %all-to-all-start) | async-done | bytes 2097184 | tf_op jit(solution)/shard_map/all_to_all | solution.py:76
  706.9 4.4 all-to-all-start.4
  711.3 2.1 convert_reduce_fusion
  713.4 0.5 multiply_convert_fusion
  713.9 0.9 copy.62
  714.7 4.4 all-to-all-done.4
  719.1 1.0 fusion
Async XLA Ops:
  7.2 2.2 copy-start
  10.5 22.4 %all-to-all-start.2 = ((bf16[4,12,4096]{2,1,0:T(8,128)(2,1)}), bf16[4,12,4096]{2,1,0:T(8,128)(2,1)S(1)}, u32[]{:S(2)}, u32[]{:S(2)}) async-start(bf16[4,12,4096]{2,1,0:T(8,128)(2,1)} %reshape.47), calls=%async_computation.2 | async-start | bytes 1048576 | tf_op jit(solution)/shard_map/all_to_all | solution.py:49
  32.9 185.8 %all-to-all-start.1 = ((bf16[1,3,128,11008]{2,1,0,3:T(4,128)(2,1)}), bf16[1,3,128,11008]{2,1,0,3:T(4,128)(2,1)}, u32[]{:S(2)}, u32[]{:S(2)}) async-start(bf16[1,3,128,11008]{2,1,0,3:T(4,128)(2,1)} %copy.55), calls=%async_computation.1 | async-start | bytes 22544384 | tf_op jit(solution)/shard_map/all_to_all | solution.py:34
  224.7 222.6 %all-to-all-start.3 = ((bf16[32,48,4096]{2,1,0:T(8,128)(2,1)}), bf16[32,48,4096]{2,1,0:T(8,128)(2,1)}, u32[]{:S(2)}, u32[]{:S(2)}) async-start(bf16[32,48,4096]{2,1,0:T(8,128)(2,1)} %stack.3), calls=%async_computation.3 | async-start | bytes 25165824 | tf_op jit(solution)/shard_map/all_to_all | solution.py:51
  257.2 361.9 %reduce-scatter.4.cloned.1.call-start = ((), (), s32[]{:S(2)}) async-start(), calls=%async_computation.8 | async-start | bytes 15728640 | tf_op jit(solution)/shard_map/reduce_scatter | solution.py:14
  477.4 182.2 %copy-start.1 = (bf16[1,2,4096,128]{3,2,1,0:T(8,128)(2,1)S(1)}, bf16[1,2,4096,128]{3,2,1,0:T(8,128)(2,1)}, u32[]{:S(2)}) copy-start(bf16[1,2,4096,128]{3,2,1,0:T(8,128)(2,1)} %param.5) | copy-start | bytes 6291460
  477.4 182.2 %reduce-scatter.6.cloned.1.call-start = ((), (), s32[]{:S(2)}) async-start(), calls=%async_computation.9 | async-start | bytes 3932160 | tf_op jit(solution)/shard_map/reduce_scatter | solution.py:14
  619.2 64.1 %reduce-scatter.8.cloned.1.call-start = ((), (), s32[]{:S(2)}) async-start(), calls=%async_computation.10 | async-start | bytes 1179648 | tf_op jit(solution)/shard_map/reduce_scatter | solution.py:14
  677.7 4.5 copy-start.2
  677.7 29.1 %all-to-all-start = ((bf16[1,2,4096,128]{3,1,0,2:T(2,128)(2,1)}), bf16[1,2,4096,128]{3,1,0,2:T(2,128)(2,1)S(1)}, u32[]{:S(2)}, u32[]{:S(2)}) async-start(bf16[1,2,4096,128]{3,1,0,2:T(2,128)(2,1)} %copy.54), calls=%async_computation | async-start | bytes 4194304 | tf_op jit(solution)/shard_map/all_to_all | solution.py:76
  706.9 12.3 %all-to-all-start.4 = ((bf16[4,12,4096]{2,1,0:T(8,128)(2,1)}), bf16[4,12,4096]{2,1,0:T(8,128)(2,1)S(1)}, u32[]{:S(2)}, u32[]{:S(2)}) async-start(bf16[4,12,4096]{2,1,0:T(8,128)(2,1)} %reshape.49), calls=%async_computation.7 | async-start | bytes 1048576 | tf_op jit(solution)/shard_map/all_to_all | solution.py:69
Sparse Core Ops, SparseCore 0:
  477.5 141.6 reduce-scatter.3
  621.6 37.9 reduce-scatter.5
  661.9 21.3 reduce-scatter.7
